TPU v7x, 256 devices: a whole 4x4x8 slice. The times are simulated.
256 devices in a mesh: row: 8 (over y, core), col: 32 (over z, x).
Axes of the slice: x: 4, y: 4, z: 8, core: 2. Of those that a mesh axis runs over, the one named last changes fastest.
Arguments:
- residuals: bfloat16 [131072, 32], P(('row', 'col')), may hold values from -6 to 6
- intersect_blocks: int32 [256, 4], P(('row', 'col')), may hold values from 0 to 3
- local_inverse: bfloat16 [131072, 1024], P(('row', 'col')), may hold values from -0.1875 to 0.1875
- coarse_basis: float32 [262144, 64], P(('row', 'col')), may hold values from -0.1875 to 0.1875
- coarse_slots: int32 [16384], replicated, may hold values from 0 to 16383, each once
- coarse_inverse: float32 [16384, 16384], P('row', 'col'), may hold values from -0.1875 to 0.1875
Outputs:
- preconditioned: float32 [131072, 32], P(('row', 'col'))
Inputs may be any that keep to these rules, and one draw needn't show every extreme that they name: `intersect_blocks`: each entry names one of the four owned blocks. `coarse_slots`: every coarse index from 0 to 16383 appears exactly once.
All inputs are finite; a program needn't handle non-finite values.
Results may differ from a plain program's by a relative error of at most 0.0003.
Values may be sent and summed in bfloat16 or wider, within the bound.
A program may use at most 64 MiB of HBM per device.

v0:
```python
import jax
import jax.numpy as jnp
from jax import lax
from jax.sharding import Mesh
from jax.sharding import PartitionSpec as P

BLK = 128
ROW_COL = ("row_0", "row_1", "col_0", "col_1")
ROW = ("row_0", "row_1")
COL = ("col_0", "col_1")


def extended(shard, sides, width, wrap):
    edges = {}
    for axis, dim in sides:
        peers, length = lax.axis_size(axis), shard.shape[dim]
        up = [(i, (i + 1) % peers) for i in range(peers if wrap else peers - 1)]
        last = lax.slice_in_dim(shard, length - width, length, axis=dim)
        first = lax.slice_in_dim(shard, 0, width, axis=dim)
        edges[dim] = lax.ppermute(last, axis, up), lax.ppermute(
            first, axis, [(b, a) for a, b in up]
        )
    done = []
    for _, dim in sides:
        low, high = edges[dim]
        around = [(width, width) if d in done else (0, 0) for d in range(shard.ndim)]
        shard = jnp.concatenate([jnp.pad(low, around), shard, jnp.pad(high, around)], axis=dim)
        done.append(dim)
    return shard


def folded(slab, axis, dim):

    def gathered(part):
        return lax.all_gather(part, axis, axis=dim, tiled=True)

    return jax.tree.map(gathered, slab)


def padded_to(lines, peers):
    spare = -len(lines) % peers
    return jnp.pad(lines, [(0, spare)] + [(0, 0)] * (lines.ndim - 1))


def own_block(pieces, axes, turns):
    shape = [lax.axis_size(a) for a in axes]
    pieces = pieces.reshape(*shape, *pieces.shape[1:])
    pieces = pieces.transpose(*turns, *range(len(axes), pieces.ndim))
    pieces = pieces.reshape(-1, *pieces.shape[len(axes) :])
    for k in turns:
        pieces = lax.psum_scatter(pieces, axes[k], scatter_dimension=0, tiled=True)
    return pieces[0]


def gather_in_order(shard, axes, turns):
    pieces = shard
    for k in turns:
        pieces = lax.all_gather(pieces, axes[k])
    done = turns[::-1]
    back = [done.index(k) for k in range(len(axes))]
    pieces = pieces.transpose(*back, *range(len(axes), pieces.ndim))
    return pieces.reshape(-1, *shard.shape)


def sum_by_parts(shard, axes, turns):
    peers, lines = lax.axis_size(axes), shard.reshape(-1, *shard.shape[1:][-1:])
    pieces = padded_to(lines, peers).reshape(peers, -1, *lines.shape[1:])
    own = own_block(pieces, axes, turns)
    whole = gather_in_order(own, axes, turns[::-1]).reshape(-1, *lines.shape[1:])
    return whole[: len(lines)].reshape(shard.shape)


def in_order(pieces, dim):
    shape = list(pieces.shape[1:])
    shape[dim] *= pieces.shape[0]
    return jnp.moveaxis(pieces, 0, dim).reshape(shape)


def whole_of(shard, axes, turns, dim):
    return in_order(gather_in_order(shard, axes, turns), dim)


def local(residuals, intersect_blocks, local_inverse, coarse_basis, coarse_slots, coarse_inverse):
    own_rows = residuals.shape[0]
    rhs_count = residuals.shape[1]
    nev_count = coarse_basis.shape[1]
    blocks = residuals.reshape(own_rows // BLK, BLK, rhs_count)
    send_index = intersect_blocks[0]
    outgoing = jnp.take(blocks, send_index, axis=0)
    padded = extended(outgoing[None, None], ((ROW, 0), (COL, 1)), 1, False)
    incoming = jnp.stack([padded[0, 1, 0], padded[2, 1, 1], padded[1, 0, 2], padded[1, 2, 3]])
    local_vec = jnp.concatenate([residuals, incoming.reshape(-1, rhs_count)], axis=0)
    schwarz = jnp.dot(local_inverse, local_vec, preferred_element_type=jnp.float32)
    partial_sums = jnp.dot(
        coarse_basis.T, local_vec.astype(jnp.float32), precision=lax.Precision.HIGHEST
    )
    column_width = coarse_inverse.shape[1]
    col_offset = lax.axis_index(COL) * column_width

    def add_piece(carry, piece):
        shifted = lax.slice_in_dim(coarse_slots, 0, piece.shape[0], axis=0) - col_offset
        inside = (shifted >= 0) & (shifted < column_width)
        target = jnp.where(inside, shifted, column_width)
        return carry.at[target].add(piece, mode="drop")

    column_part = add_piece(
        jnp.zeros((column_width, rhs_count), jnp.float32), folded(partial_sums, ROW_COL, 0)
    )
    product = jnp.dot(coarse_inverse, column_part, precision=lax.Precision.HIGHEST)
    row_total = sum_by_parts(product, COL, (0, 1))
    whole_coarse = whole_of(row_total, ROW, (0, 1), 0)
    my_slots = lax.dynamic_slice_in_dim(
        coarse_slots, lax.axis_index(ROW_COL) * nev_count, nev_count, 0
    )
    own_coarse = jnp.take(whole_coarse, my_slots, axis=0)
    prolonged = jnp.dot(coarse_basis, own_coarse, precision=lax.Precision.HIGHEST)
    returning = prolonged[own_rows:].reshape(-1, BLK, rhs_count)
    padded_back = extended(returning[None, None], ((ROW, 0), (COL, 1)), 1, False)
    returned = jnp.stack(
        [padded_back[2, 1, 0], padded_back[0, 1, 1], padded_back[1, 2, 2], padded_back[1, 0, 3]]
    )
    matches = (send_index[:, None] == jnp.arange(own_rows // BLK, dtype=jnp.int32)[None, :]).astype(
        jnp.float32
    )
    added = jnp.einsum("db,dkr->bkr", matches, returned, precision=lax.Precision.HIGHEST)
    return schwarz + prolonged[:own_rows] + added.reshape(own_rows, rhs_count)


def solution(mesh):
    torus = Mesh(mesh.devices.reshape(4, 2, 8, 4), ("row_0", "row_1", "col_0", "col_1"))
    in_specs = (
        P(ROW_COL, None),
        P(ROW_COL, None),
        P(ROW_COL, None),
        P(ROW_COL, None),
        P(),
        P(ROW, COL),
    )
    out_specs = P(ROW_COL, None)
    return jax.shard_map(local, mesh=torus, in_specs=in_specs, out_specs=out_specs, check_vma=False)
```

profile of v0, /device:TPU:1, one launch (start us, length us, event | category | flops | bytes accessed | tf_op | source)
XLA Modules:
  0.0 423.2 jit_solution(14299290129409189344)
XLA Ops:
  6.5 0.7 fusion.18
  7.3 0.7 compare_and_fusion.1
  7.9 0.8 copy_bitcast_fusion
  8.7 0.8 compare_and_fusion
  9.5 0.6 gather_fusion
  10.1 1.3 collective-permute-start.3
  11.4 4.6 %collective-permute-start.2 = (bf16[1,1,4,128,32]{3,4,2,1,0:T(8,128)(2,1)S(1)}, bf16[1,1,4,128,32]{3,4,2,1,0:T(8,128)(2,1)S(1)}, u32[]{:S(2)}, u32[]{:S(2)}) collective-permute-start(bf16[1,1,4,128,32]{3,4,2,1,0:T(8,128)(2,1)S(1)} %bitcast_select_fusion), channel_id=1, source_target_pairs={{0,1},{1,2},{2,3},{3,4},{4,5},{5,6},{6,7},{7,8},{8,9},{9,10},{10,1... | collective-permute-start | bytes 98312 | tf_op jit(solution)/shard_map/ppermute | solution.py:20
  16.0 5.1 %collective-permute-start.1 = (bf16[1,1,4,128,32]{3,4,2,1,0:T(8,128)(2,1)S(1)}, bf16[1,1,4,128,32]{3,4,2,1,0:T(8,128)(2,1)S(1)}, u32[]{:S(2)}, u32[]{:S(2)}) collective-permute-start(bf16[1,1,4,128,32]{3,4,2,1,0:T(8,128)(2,1)S(1)} %bitcast_select_fusion), channel_id=1, source_target_pairs={{32,0},{64,32},{96,64},{128,96},{160,128},{192,160},{224,192},{33,... | collective-permute-start | bytes 98312 | tf_op jit(solution)/shard_map/ppermute | solution.py:20
  21.1 1.9 collective-permute-start
  23.0 0.8 constant_dynamic-update-slice_fusion
  24.2 1.8 convolution_bitcast_fusion.3
  26.1 0.9 compare_select_fusion
  26.9 120.1 %all-gather.11.cloned.1.call-done = f32[256,64,32]{1,2,0:T(8,128)} async-done(((f32[1,64,32]{1,2,0:T(8,128)}), f32[256,64,32]{1,2,0:T(8,128)}) %all-gather.11.cloned.1.call-update) | async-done | bytes 2097168 | tf_op jit(solution)/shard_map/all_gather | solution.py:35
  147.0 6.9 %copy.51 = f32[256,64,32]{2,1,0:T(8,128)} copy(f32[256,64,32]{1,2,0:T(8,128)} %all-gather.11.cloned.1.call-done) | data formatting | bytes 4194304
  154.0 87.7 %scatter_custom_fusion = f32[512,32]{1,0:T(8,128)S(1)} fusion(s32[16384]{0:T(1024)S(1)} %compare_select_fusion, f32[16384,32]{1,0:T(8,128)} %bitcast.71, f32[]{:T(128)} %constant.60.clone.1), kind=kCustom, calls=%fused_computation.10 | custom fusion | flops 524288 | bytes 66048 | tf_op jit(solution)/shard_map/scatter-add | solution.py:104
  241.6 6.2 %convolution_bitcast_fusion = f32[2048,32]{0,1:T(8,128)S(1)} fusion(f32[512,32]{1,0:T(8,128)S(1)} %scatter_custom_fusion, f32[2048,512]{1,0:T(8,128)} %param.11), kind=kOutput, calls=%fused_computation.3 | convolution fusion | flops 402653184 | bytes 4521984 | tf_op jit(solution)/shard_map/dot_general | solution.py:109
  248.0 1.1 copy.44
  249.2 29.9 %reduce-scatter.3.cloned.1.call-done = f32[4,64,32]{1,2,0:T(8,128)} async-done(((f32[32,64,32]{1,2,0:T(8,128)}), f32[4,64,32]{1,2,0:T(8,128)}) %reduce-scatter.3.cloned.1.call-update) | async-done | bytes 32784 | tf_op jit(solution)/shard_map/reduce_scatter | solution.py:51
  279.2 26.6 %reduce-scatter.5.cloned.1.call-done = f32[1,64,32]{1,2,0:T(8,128)} async-done(((f32[4,64,32]{1,2,0:T(8,128)}), f32[1,64,32]{1,2,0:T(8,128)}) %reduce-scatter.5.cloned.1.call-update) | async-done | bytes 8208 | tf_op jit(solution)/shard_map/reduce_scatter | solution.py:51
  305.8 9.2 %all_gather.22 = f32[4,64,32]{1,2,0:T(8,128)S(1)} all-gather(f32[1,64,32]{1,2,0:T(8,128)} %reduce-scatter.5.cloned.1.call-done), channel_id=1, replica_groups=mesh['row_0'=4,'row_1'=2,'col_0'=8,'col_1'=4] {'col_1'}, dimensions={0}, use_global_device_ids=true | all-gather | bytes 40960 | tf_op jit(solution)/shard_map/all_gather | solution.py:58
  315.0 20.7 %all-gather = f32[32,64,32]{1,2,0:T(8,128)S(1)} all-gather(f32[4,64,32]{1,2,0:T(8,128)S(1)} %all_gather.22), channel_id=2, replica_groups=mesh['row_0'=4,'row_1'=2,'col_0'=8,'col_1'=4] {'col_0'}, dimensions={0}, use_global_device_ids=true | all-gather | bytes 294912 | tf_op jit(solution)/shard_map/all_gather | solution.py:58
  336.0 0.9 all_gather_reshape_reshape.3
  336.9 34.1 %all-gather.7.cloned.1.call-done = f32[4,2048,32]{1,2,0:T(8,128)} async-done(((f32[1,2048,32]{1,2,0:T(8,128)}), f32[4,2048,32]{1,2,0:T(8,128)}) %all-gather.7.cloned.1.call-update) | async-done | bytes 1048592 | tf_op jit(solution)/shard_map/all_gather | solution.py:58
  371.1 21.0 %all-gather.9.cloned.1.call-done = f32[8,2048,32]{1,2,0:T(8,128)} async-done(((f32[4,2048,32]{1,2,0:T(8,128)}), f32[8,2048,32]{1,2,0:T(8,128)}) %all-gather.9.cloned.1.call-update) | async-done | bytes 2097168 | tf_op jit(solution)/shard_map/all_gather | solution.py:58
  392.1 6.3 %copy.46 = f32[4,2,2048,32]{3,2,1,0:T(8,128)} copy(f32[4,2,2048,32]{2,3,0,1:T(8,128)} %bitcast.72) | data formatting | bytes 4194304 | tf_op jit(solution)/shard_map/transpose | solution.py:61
  398.4 4.0 gather_fusion.1
  402.8 2.1 collective-permute-start.4
  405.0 3.4 collective-permute-start.5
  408.4 1.3 collective-permute-start.6
  409.7 4.0 collective-permute-start.7
  413.8 1.5 collective-permute-done.7
  415.6 1.1 fusion.1
  (41 shorter events, 1.9 us)
Async XLA Ops:
  6.5 409.0 %copy-start = (bf16[512,1024]{1,0:T(8,128)(2,1)S(1)}, bf16[512,1024]{1,0:T(8,128)(2,1)}, u32[]{:S(2)}) copy-start(bf16[512,1024]{1,0:T(8,128)(2,1)} %param.8) | copy-start | bytes 3145732
  6.5 140.5 %all-gather.11.cloned.1.call-start = ((), (), s32[]{:S(2)}) async-start(), calls=%async_computation.6 | async-start | bytes 4210688 | tf_op jit(solution)/shard_map/all_gather | solution.py:35
  10.1 13.6 %collective-permute-start.3 = (bf16[1,1,4,128,32]{3,4,2,1,0:T(8,128)(2,1)S(1)}, bf16[1,1,4,128,32]{3,4,2,1,0:T(8,128)(2,1)S(1)}, u32[]{:S(2)}, u32[]{:S(2)}) collective-permute-start(bf16[1,1,4,128,32]{3,4,2,1,0:T(8,128)(2,1)S(1)} %bitcast_select_fusion), channel_id=1, source_target_pairs={{1,0},{2,1},{3,2},{4,3},{5,4},{6,5},{7,6},{8,7},{9,8},{10,9},{11,1... | collective-permute-start | bytes 98312 | tf_op jit(solution)/shard_map/ppermute | solution.py:20
  11.4 12.3 %collective-permute-start.2 = (bf16[1,1,4,128,32]{3,4,2,1,0:T(8,128)(2,1)S(1)}, bf16[1,1,4,128,32]{3,4,2,1,0:T(8,128)(2,1)S(1)}, u32[]{:S(2)}, u32[]{:S(2)}) collective-permute-start(bf16[1,1,4,128,32]{3,4,2,1,0:T(8,128)(2,1)S(1)} %bitcast_select_fusion), channel_id=1, source_target_pairs={{0,1},{1,2},{2,3},{3,4},{4,5},{5,6},{6,7},{7,8},{8,9},{9,10},{10,1... | collective-permute-start | bytes 98312 | tf_op jit(solution)/shard_map/ppermute | solution.py:20
  16.0 7.8 %collective-permute-start.1 = (bf16[1,1,4,128,32]{3,4,2,1,0:T(8,128)(2,1)S(1)}, bf16[1,1,4,128,32]{3,4,2,1,0:T(8,128)(2,1)S(1)}, u32[]{:S(2)}, u32[]{:S(2)}) collective-permute-start(bf16[1,1,4,128,32]{3,4,2,1,0:T(8,128)(2,1)S(1)} %bitcast_select_fusion), channel_id=1, source_target_pairs={{32,0},{64,32},{96,64},{128,96},{160,128},{192,160},{224,192},{33,... | collective-permute-start | bytes 98312 | tf_op jit(solution)/shard_map/ppermute | solution.py:20
  21.1 3.1 collective-permute-start
  26.0 253.1 %reduce-scatter.3.cloned.1.call-start = ((), (), s32[]{:S(2)}) async-start(), calls=%async_computation.2 | async-start | bytes 589824 | tf_op jit(solution)/shard_map/reduce_scatter | solution.py:51
  249.2 56.6 %reduce-scatter.5.cloned.1.call-start = ((), (), s32[]{:S(2)}) async-start(), calls=%async_computation.3 | async-start | bytes 81920 | tf_op jit(solution)/shard_map/reduce_scatter | solution.py:51
  279.1 91.9 %all-gather.7.cloned.1.call-start = ((), (), s32[]{:S(2)}) async-start(), calls=%async_computation.4 | async-start | bytes 1310720 | tf_op jit(solution)/shard_map/all_gather | solution.py:58
  336.9 55.2 %all-gather.9.cloned.1.call-start = ((), (), s32[]{:S(2)}) async-start(), calls=%async_computation.5 | async-start | bytes 3145728 | tf_op jit(solution)/shard_map/all_gather | solution.py:58
  392.1 10.3 %copy-start.1 = (f32[1024,64]{0,1:T(8,128)S(1)}, f32[1024,64]{0,1:T(8,128)}, u32[]{:S(2)}) copy-start(f32[1024,64]{0,1:T(8,128)} %param.9) | copy-start | bytes 786436
  392.1 23.2 %copy-start.2 = (s32[1,4]{1,0:T(1,128)S(1)}, s32[1,4]{1,0:T(1,128)}, u32[]{:S(2)}) copy-start(s32[1,4]{1,0:T(1,128)} %param.7) | copy-start | bytes 52
  402.8 10.9 %collective-permute-start.4 = (f32[1,1,4,128,32]{3,4,2,1,0:T(8,128)S(1)}, f32[1,1,4,128,32]{3,4,2,1,0:T(8,128)S(1)}, u32[]{:S(2)}, u32[]{:S(2)}) collective-permute-start(f32[1,1,4,128,32]{3,4,2,1,0:T(8,128)S(1)} %copy.47), channel_id=1, source_target_pairs={{32,0},{64,32},{96,64},{128,96},{160,128},{192,160},{224,192},{33,... | collective-permute-start | bytes 196616 | tf_op jit(solution)/shard_map/ppermute | solution.py:20
  405.0 8.8 %collective-permute-start.5 = (f32[1,1,4,128,32]{3,4,2,1,0:T(8,128)S(1)}, f32[1,1,4,128,32]{3,4,2,1,0:T(8,128)S(1)}, u32[]{:S(2)}, u32[]{:S(2)}) collective-permute-start(f32[1,1,4,128,32]{3,4,2,1,0:T(8,128)S(1)} %copy.47), channel_id=1, source_target_pairs={{0,32},{32,64},{64,96},{96,128},{128,160},{160,192},{192,224},{1,3... | collective-permute-start | bytes 196616 | tf_op jit(solution)/shard_map/ppermute | solution.py:20
  408.4 5.3 %collective-permute-start.6 = (f32[1,1,4,128,32]{3,4,2,1,0:T(8,128)S(1)}, f32[1,1,4,128,32]{3,4,2,1,0:T(8,128)S(1)}, u32[]{:S(2)}, u32[]{:S(2)}) collective-permute-start(f32[1,1,4,128,32]{3,4,2,1,0:T(8,128)S(1)} %copy.47), channel_id=1, source_target_pairs={{1,0},{2,1},{3,2},{4,3},{5,4},{6,5},{7,6},{8,7},{9,8},{10,9},{11,1... | collective-permute-start | bytes 196616 | tf_op jit(solution)/shard_map/ppermute | solution.py:20
  409.7 5.6 %collective-permute-start.7 = (f32[1,1,4,128,32]{3,4,2,1,0:T(8,128)S(1)}, f32[1,1,4,128,32]{3,4,2,1,0:T(8,128)S(1)}, u32[]{:S(2)}, u32[]{:S(2)}) collective-permute-start(f32[1,1,4,128,32]{3,4,2,1,0:T(8,128)S(1)} %copy.47), channel_id=1, source_target_pairs={{0,1},{1,2},{2,3},{3,4},{4,5},{5,6},{6,7},{7,8},{8,9},{9,10},{10,1... | collective-permute-start | bytes 196616 | tf_op jit(solution)/shard_map/ppermute | solution.py:20
Sparse Core Ops, SparseCore 0:
  26.1 120.8 all-gather.10
  249.3 29.7 reduce-scatter.2
  281.6 24.1 reduce-scatter.4
  337.0 34.0 all-gather.6
  372.7 19.3 all-gather.8
where the time goes:
time: 428 us; the launch traced here: 423 us
  waiting for transfers between devices  234 us (55%)
  other arithmetic  90.8 us (21%)
  blocking collectives  29.8 us (7%)
  starting transfers between devices  23.8 us (6%)
  local copies, waits for them, and re-layouts  21.9 us (5%)
  between operations  13.4 us (3%)
  matrix products  9.66 us (2%)
    all_gather x1, waiting for transfers between devices, gathered(): return lax.all_gather(part, axis, axis=dim, tiled=True)  120 us
    scatter-add x1, other arithmetic, add_piece(): return carry.at[target].add(piece, mode='drop')  87.7 us
    reduce_scatter x2, waiting for transfers between devices, own_block(): pieces = lax.psum_scatter(pieces, axes[k], scatter_dimension=0, tiled=True)  56.5 us
    all_gather x2, waiting for transfers between devices, gather_in_order(): pieces = lax.all_gather(pieces, axes[k])  55.1 us
    all_gather x2, blocking collectives, gather_in_order(): pieces = lax.all_gather(pieces, axes[k])  29.8 us
    ppermute x4, starting transfers between devices, extended(): lax.ppermute(last, axis, up)  13.9 us
    ppermute x4, starting transfers between devices, extended(): lax.ppermute(first, axis, [(b, a) for a, b in up])  9.76 us
  transfers between devices with their start and end apart: 13, of which 7 were waited for; matrix products, arithmetic and copies ran while one was open for 0% of the time, Pallas kernels for 0%

commit v1 on v0

v1 whole, which is shorter than its diff:
```python
import functools

import jax
import jax.numpy as jnp
from jax import lax
from jax.experimental import pallas as pl
from jax.experimental.pallas import tpu as pltpu
from jax.sharding import Mesh
from jax.sharding import PartitionSpec as P

MESH = pl.DeviceIdType.MESH
AXES = ("row_0", "row_1", "col_0", "col_1")
ROW_COL = AXES
ROW = AXES[:2]
COL = AXES[2:]
NY, NK, NZ, NX = 4, 2, 8, 4
NR = NY * NK
BLK = 128
OWN = 512
LOC = 1024
NEV = 64
RHS = 32
LANES = 128
PART = 2048
CHUNKS = 2
WIDTH = PART // CHUNKS
ROWS = WIDTH // LANES
F32 = jnp.float32
BF16 = jnp.bfloat16
NT = (((1,), (1,)), ((), ()))


def dot(a, b):
    return jnp.dot(a, b, preferred_element_type=F32)


def dot_nt(a, b):
    return lax.dot_general(a, b, NT, preferred_element_type=F32)


def halves(x):
    high = x.astype(BF16)
    return high, (x - high.astype(F32)).astype(BF16)


def kernel(
    ib, resid, slots, basis_hbm, linv_hbm, cinv_hbm, out,
    basis, linv, cinv, chigh, clow, bstack, locvec, hout, hin, psend, precv, table, pick1, pick2,
    gsend, grecv, xsend, xrecv, zsend, zrecv, table2, osend, orecv, rsend, rrecv,
    load_sem, send_sem, recv_sem, xsem,
):
    y, k, z, x = (lax.axis_index(a) for a in AXES)
    r = y * NK + k
    c = z * NX + x

    def at_rx(r2, x2):
        return (lax.div(r2, NK), lax.rem(r2, NK), z, x2)

    def at_zx(z2, x2):
        return (y, k, z2, x2)

    def same_z_peer(p):
        peer = lax.rem(r * NX + x + p, NR * NX)
        return lax.div(peer, NX), lax.rem(peer, NX)

    def same_row_peer(p):
        peer = lax.rem(c + p, NZ * NX)
        return lax.div(peer, NX), lax.rem(peer, NX)

    def send(stage, src, dst, where, sem=None):
        pltpu.make_async_remote_copy(
            src_ref=src, dst_ref=dst, send_sem=send_sem.at[stage], recv_sem=recv_sem.at[stage] if sem is None else sem,
            device_id=where, device_id_type=MESH,
        ).start()

    def landed(ref, sem):
        pltpu.make_async_copy(ref, ref, sem).wait()

    loads = [
        pltpu.make_async_copy(basis_hbm, basis, load_sem.at[0]),
        pltpu.make_async_copy(cinv_hbm, cinv, load_sem.at[1]),
        pltpu.make_async_copy(linv_hbm, linv, load_sem.at[2]),
    ]
    barrier = pltpu.get_barrier_semaphore()

    @pl.loop(1, NR * NX)
    def _(p):
        r2, x2 = same_z_peer(p)
        pl.semaphore_signal(barrier, inc=1, device_id=at_rx(r2, x2), device_id_type=MESH)

    @pl.loop(0, (NZ - 1) * NX)
    def _(p):
        z2 = lax.rem(z + 1 + lax.div(p, NX), NZ)
        pl.semaphore_signal(barrier, inc=1, device_id=at_zx(z2, lax.rem(p, NX)), device_id_type=MESH)

    for load in loads:
        load.start()

    blocks = [resid[:, b * BLK:(b + 1) * BLK] for b in range(OWN // BLK)]
    for d in range(4):
        which = ib[0, d]
        block = blocks[0]
        for b in range(1, OWN // BLK):
            block = jnp.where(which == b, blocks[b], block)
        hout[d] = block
    locvec[:, :OWN] = resid[...]

    sub = lax.broadcasted_iota(jnp.int32, (LANES, LANES), 0)
    sub16 = lax.broadcasted_iota(jnp.int32, (16, LANES), 0)
    lane16 = lax.broadcasted_iota(jnp.int32, (16, LANES), 1).astype(F32)

    def invert(g, total):
        rows = slots[pl.ds(g * 8, 8), :]
        low = rows & (LANES - 1)
        high = lax.shift_right_logical(rows, 7) - z * 16
        picks, values = [], []
        for u in range(8):
            entry = g * 8 + u
            row = lax.rem(lax.div(entry, 2), NZ) * 16 + lax.div(entry, 16) * 2 + (u & 1)
            picks.append((low[u:u + 1] == sub).astype(F32).astype(BF16))
            here = high[u:u + 1] == sub16
            values.append(jnp.concatenate(
                [jnp.where(here, row.astype(F32), 0.0), jnp.where(here, lane16, 0.0)], axis=0).astype(BF16))
        return total + dot_nt(jnp.concatenate(picks, axis=1), jnp.concatenate(values, axis=1))

    inverse = lax.fori_loop(0, 16, invert, jnp.zeros((LANES, 32), F32)).T.astype(jnp.int32)
    from_row, from_lane = inverse[:16], inverse[16:]
    my_slots = slots[pl.ds(r * 16, 16), :]
    want_row, want_lane = lax.shift_right_logical(my_slots, 7), my_slots & (LANES - 1)
    for a in range(16):
        for pick, row in ((pick1, from_row), (pick2, want_row)):
            hot = (row[a:a + 1] == sub).astype(F32).astype(BF16)
            pick[:LANES, a * LANES:(a + 1) * LANES] = hot
            pick[LANES:, a * LANES:(a + 1) * LANES] = hot

    def gather(source, pick, lane):
        high, low = halves(source.T)
        stacked = jnp.concatenate([high, low], axis=1)
        rows = []
        for a in range(0, 16, 2):
            picked = dot(stacked, pick[:, a * LANES:(a + 2) * LANES])
            for h in range(2):
                mine = lane[a + h:a + h + 1] == sub
                rows.append(jnp.sum(jnp.where(mine, picked[:, h * LANES:(h + 1) * LANES], 0.0), axis=0, keepdims=True))
        return jnp.concatenate(rows, axis=0)

    loads[0].wait()
    bhigh, blow = halves(basis[...])
    bstack[0:NEV] = bhigh
    bstack[NEV:2 * NEV] = bhigh
    bstack[2 * NEV:3 * NEV] = blow

    pl.semaphore_wait(barrier, NR * NX - 1 + (NZ - 1) * NX)

    r_up, r_down = lax.rem(r + 1, NR), lax.rem(r + NR - 1, NR)
    c_up, c_down = lax.rem(c + 1, NZ * NX), lax.rem(c + NZ * NX - 1, NZ * NX)
    sides = (
        at_rx(r_up, x), at_rx(r_down, x),
        at_zx(lax.div(c_up, NX), lax.rem(c_up, NX)), at_zx(lax.div(c_down, NX), lax.rem(c_down, NX)),
    )
    inside = (r > 0, r < NR - 1, c > 0, c < NZ * NX - 1)
    inside_back = (r < NR - 1, r > 0, c < NZ * NX - 1, c > 0)
    for d in range(4):
        send(0, hout.at[d], hin.at[d], sides[d])

    loads[1].wait()

    def split(i, _):
        rows = pl.ds(i * 64, 64)
        high, low = halves(cinv[rows, :])
        chigh[rows, :] = high
        clow[rows, :] = low
        return 0

    lax.fori_loop(0, PART // 64, split, 0)

    landed(hin, recv_sem.at[0])
    for d in range(4):
        locvec[:, OWN + d * BLK:OWN + (d + 1) * BLK] = jnp.where(inside[d], hin[d], jnp.zeros_like(hin[d]))

    vec = locvec[...]
    low2 = jnp.concatenate([bstack[2 * NEV:], bstack[2 * NEV:]], axis=0)
    partial = dot_nt(vec, bstack[:2 * NEV]) + dot_nt(vec, low2)
    psend[...] = partial.reshape(RHS, 1, LANES)
    me = r * NX + x
    precv[pl.ds(me, 1)] = psend[pl.ds(me, 1)]

    @pl.loop(1, NR * NX)
    def _(p):
        r2, x2 = same_z_peer(p)
        send(1, psend.at[r2 * NX + x2], precv.at[me], at_rx(r2, x2))

    loads[2].wait()
    schwarz = dot_nt(vec, linv[...])
    landed(precv.at[pl.ds(0, NR * NX - 1)], recv_sem.at[1])

    got = precv[...].reshape(16, 2, LANES)
    first = lax.broadcasted_iota(jnp.int32, (16, LANES), 1) < NEV
    mine = pl.ds(pl.multiple_of(z * 16, 16), 16)
    table[mine, :] = jnp.where(first, got[:, 0], got[:, 1])

    @pl.loop(1, NZ)
    def _(p):
        send(2, table.at[mine], table.at[mine], at_zx(lax.rem(z + p, NZ), x))

    landed(table.at[pl.ds(0, (NZ - 1) * 16)], recv_sem.at[2])

    gsend[...] = gather(table[...], pick1, from_lane).reshape(NX, 4, LANES)
    grecv[pl.ds(me, 1)] = gsend[pl.ds(x, 1)]

    @pl.loop(1, NR * NX)
    def _(p):
        r2, x2 = same_z_peer(p)
        send(3, gsend.at[x2], grecv.at[me], at_rx(r2, x2))

    landed(grecv.at[pl.ds(0, NR * NX - 1)], recv_sem.at[3])

    rhigh, rlow = halves(jnp.concatenate([grecv[:, a, :] for a in range(4)], axis=1))
    both = jnp.concatenate([rhigh, rlow], axis=0)
    for n in range(CHUNKS):
        def product(i, _):
            cols = pl.ds(n * WIDTH + i * 256, 256)
            top = dot_nt(both, chigh[cols, :])
            part = top[:RHS] + top[RHS:] + dot_nt(rhigh, clow[cols, :])
            xsend[n, :, :, pl.ds(pl.multiple_of(i * 256, 256), 256)] = part.reshape(NX, NZ, 256)
            return 0

        lax.fori_loop(0, WIDTH // 256, product, 0)

        @pl.loop(1, NX)
        def _(p):
            x2 = lax.rem(x + p, NX)
            send(4, xsend.at[n, x2], xrecv.at[n, p - 1], at_zx(z, x2), xsem.at[n])

    for n in range(CHUNKS):
        landed(xrecv.at[n], xsem.at[n])
        total = xsend[n, pl.ds(x, 1)][0]
        for p in range(NX - 1):
            total = total + xrecv[n, p]
        for j in range(ROWS):
            zsend[n, :, j, :] = total[:, j * LANES:(j + 1) * LANES]

        @pl.loop(1, NZ)
        def _(p):
            z2 = lax.rem(z + p, NZ)
            send(5, zsend.at[n, z2], zrecv.at[p - 1, n], at_zx(z2, x))

    landed(zrecv, recv_sem.at[5])
    mine2 = pl.ds(pl.multiple_of(r * 16, 16), 16)
    total = zsend[:, pl.ds(z, 1)].reshape(16, LANES)
    for p in range(NZ - 1):
        total = total + zrecv[p].reshape(16, LANES)
    table2[mine2, :] = total

    @pl.loop(1, NR)
    def _(p):
        send(6, table2.at[mine2], table2.at[mine2], at_rx(lax.rem(r + p, NR), x))

    landed(table2.at[pl.ds(0, (NR - 1) * 16)], recv_sem.at[6])

    osend[...] = gather(table2[...], pick2, want_lane).reshape(16, 1, LANES)
    q = x * NZ + z
    orecv[pl.ds(q, 1)] = osend[pl.ds(lax.div(c, 2), 1)]

    @pl.loop(1, NZ * NX)
    def _(p):
        z2, x2 = same_row_peer(p)
        send(7, osend.at[z2 * 2 + lax.div(x2, 2)], orecv.at[q], at_zx(z2, x2))

    landed(orecv.at[pl.ds(0, NZ * NX - 1)], recv_sem.at[7])
    entries = orecv[...].reshape(RHS, LANES)
    high, low = halves(jnp.where(lax.rem(x, 2) == 1, entries[:, NEV:], entries[:, :NEV]))
    coarse = jnp.concatenate([high, low, high], axis=1)

    back = dot(coarse, bstack[:, OWN:])
    for d in range(4):
        rsend[d] = back[:, d * BLK:(d + 1) * BLK]
    opposite = (1, 0, 3, 2)
    for d in range(4):
        send(8, rsend.at[d], rrecv.at[d], sides[opposite[d]])
    result = schwarz + dot(coarse, bstack[:, :OWN])
    landed(rrecv, recv_sem.at[8])
    parts = [result[:, b * BLK:(b + 1) * BLK] for b in range(OWN // BLK)]
    for d in range(4):
        returned = jnp.where(inside_back[d], rrecv[d], jnp.zeros_like(rrecv[d]))
        which = ib[0, d]
        for b in range(OWN // BLK):
            parts[b] = parts[b] + jnp.where(which == b, returned, jnp.zeros_like(returned))
    for b in range(OWN // BLK):
        out[:, b * BLK:(b + 1) * BLK] = parts[b]

    for stage, ref in (
        (0, hout), (1, psend.at[pl.ds(0, NR * NX - 1)]), (2, table.at[pl.ds(0, (NZ - 1) * 16)]),
        (3, grecv.at[pl.ds(0, NR * NX - 1)]), (4, xrecv), (5, zrecv), (6, table2.at[pl.ds(0, (NR - 1) * 16)]),
        (7, orecv.at[pl.ds(0, NZ * NX - 1)]), (8, rsend),
    ):
        landed(ref, send_sem.at[stage])


def local(residuals, intersect_blocks, local_inverse, coarse_basis, coarse_slots, coarse_inverse):
    vmem = pl.BlockSpec(memory_space=pltpu.VMEM)
    hbm = pl.BlockSpec(memory_space=pl.ANY)
    result = pl.pallas_call(
        kernel,
        out_shape=jax.ShapeDtypeStruct((RHS, OWN), F32),
        in_specs=[pl.BlockSpec(memory_space=pltpu.SMEM), vmem, vmem, hbm, hbm, hbm],
        out_specs=vmem,
        scratch_shapes=[
            pltpu.VMEM((NEV, LOC), F32),
            pltpu.VMEM((OWN, LOC), BF16),
            pltpu.VMEM((PART, OWN), F32),
            pltpu.VMEM((PART, OWN), BF16),
            pltpu.VMEM((PART, OWN), BF16),
            pltpu.VMEM((3 * NEV, LOC), BF16),
            pltpu.VMEM((RHS, LOC), BF16),
            pltpu.VMEM((4, RHS, BLK), BF16),
            pltpu.VMEM((4, RHS, BLK), BF16),
            pltpu.VMEM((RHS, 1, LANES), F32),
            pltpu.VMEM((RHS, 1, LANES), F32),
            pltpu.VMEM((LANES, LANES), F32),
            pltpu.VMEM((2 * LANES, PART), BF16),
            pltpu.VMEM((2 * LANES, PART), BF16),
            pltpu.VMEM((NX, 4, LANES), F32),
            pltpu.VMEM((RHS, 4, LANES), F32),
            pltpu.VMEM((CHUNKS, NX, NZ, WIDTH), F32),
            pltpu.VMEM((CHUNKS, NX - 1, NZ, WIDTH), F32),
            pltpu.VMEM((CHUNKS, NZ, ROWS, LANES), F32),
            pltpu.VMEM((NZ - 1, CHUNKS, ROWS, LANES), F32),
            pltpu.VMEM((LANES, LANES), F32),
            pltpu.VMEM((16, 1, LANES), F32),
            pltpu.VMEM((RHS, 1, LANES), F32),
            pltpu.VMEM((4, RHS, BLK), F32),
            pltpu.VMEM((4, RHS, BLK), F32),
            pltpu.SemaphoreType.DMA((3,)),
            pltpu.SemaphoreType.DMA((9,)),
            pltpu.SemaphoreType.DMA((9,)),
            pltpu.SemaphoreType.DMA((CHUNKS,)),
        ],
        compiler_params=pltpu.CompilerParams(collective_id=0, has_side_effects=True),
        name="schwarz",
    )(
        intersect_blocks, residuals.T, coarse_slots.reshape(LANES, LANES), coarse_basis.T, local_inverse, coarse_inverse
    )
    return result.T


def solution(mesh):
    torus = Mesh(mesh.devices.reshape(NY, NK, NZ, NX), AXES)
    in_specs = (
        P(ROW_COL, None),
        P(ROW_COL, None),
        P(ROW_COL, None),
        P(ROW_COL, None),
        P(),
        P(ROW, COL),
    )
    return jax.shard_map(local, mesh=torus, in_specs=in_specs, out_specs=P(ROW_COL, None), check_vma=False)
```

time: 428 us -> 60.3 us (0.14); the launches traced: 423 us -> 60.2 us
  waiting for transfers between devices: 234 us -> 0 us
  other arithmetic: 90.8 us -> 0 us
  Pallas kernels: 0 us -> 58.7 us
  blocking collectives: 29.8 us -> 0 us
  starting transfers between devices: 23.8 us -> 0 us
  local copies, waits for them, and re-layouts: 21.9 us -> 1.47 us
  between operations: 13.4 us -> 0.01 us
  matrix products: 9.66 us -> 0 us
    all_gather x3 -> x0, waiting for transfers between devices: 175 us -> none  [the longest x1 120 us: gathered(): return lax.all_gather(part, axis, axis=dim, tiled=True)]
    scatter-add x1 -> x0, other arithmetic: 87.7 us -> none  [add_piece(): return carry.at[target].add(piece, mode='drop')]
    pallas_call x0 -> x1, Pallas kernels: none -> 58.7 us  [local(): pl.pallas_call(kernel, out_shape=jax.ShapeDtypeStruct((RHS, OWN), F32), i...]
    reduce_scatter x2 -> x0, waiting for transfers between devices: 56.5 us -> none  [own_block(): pieces = lax.psum_scatter(pieces, axes[k], scatter_dimension=0, tiled=True)]
    all_gather x2 -> x0, blocking collectives: 29.8 us -> none  [gather_in_order(): pieces = lax.all_gather(pieces, axes[k])]
    ppermute x8 -> x0, starting transfers between devices: 23.7 us -> none  [the longest x4 13.9 us: extended(): lax.ppermute(last, axis, up)]
    dot_general x5 -> x0, matrix products: 9.66 us -> none  [the longest x1 6.17 us: local(): jnp.dot(coarse_inverse, column_part, precision=lax.Precision.HIGHEST)]
    transpose x1 -> x0, local copies, waits for them, and re-layouts: 6.31 us -> none  [gather_in_order(): pieces = pieces.transpose(*back, *range(len(axes), pieces.ndim))]
  transfers between devices with their start and end apart: 13 -> 0, of which waited for: 7 -> 0; matrix products, arithmetic and copies ran while one was open for 0% -> 0% of each run, Pallas kernels for 0% -> 0%
where the time goes in v1:
time: 60.3 us; the launch traced here: 60.2 us
  Pallas kernels  58.7 us (97%)
  local copies, waits for them, and re-layouts  1.47 us (2%)
    pallas_call x1, Pallas kernels, local(): pl.pallas_call(kernel, out_shape=jax.ShapeDtypeStruct((RHS, OWN), F32), i...  58.7 us
    unnamed x1, local copies, waits for them, and re-layouts  1.47 us

profile of v1, /device:TPU:1, one launch (start us, length us, event | category | flops | bytes accessed | tf_op | source)
XLA Modules:
  0.0 60.2 jit_solution(11605171557120136478)
XLA Ops:
  0.0 58.7 %schwarz.1 = f32[32,512]{1,0:T(8,128)} custom-call(s32[1,4]{1,0:T(1,128)} %ib.1, bf16[32,512]{1,0:T(8,128)(2,1)} %bitcast.7, s32[128,128]{1,0:T(8,128)} %bitcast.6, f32[64,1024]{1,0:T(8,128)} %bitcast.5, bf16[512,1024]{1,0:T(8,128)(2,1)} %linv_hbm.1, f32[2048,512]{1,0:T(8,128)} %cinv_hbm.1), custom_call_target="tpu_custom_call" | custom-call | tf_op jit(solution)/shard_map/schwarz/pallas_call | solution.py:303
  58.7 1.5 %copy.8 = f32[512,32]{0,1:T(8,128)} copy(f32[512,32]{0,1:T(8,128)} %bitcast.4) | data formatting | bytes 131072

commit v2 on v1

v2 whole, which is shorter than its diff:
```python
import functools

import jax
import jax.numpy as jnp
from jax import lax
from jax.experimental import pallas as pl
from jax.experimental.pallas import tpu as pltpu
from jax.sharding import Mesh
from jax.sharding import PartitionSpec as P

MESH = pl.DeviceIdType.MESH
AXES = ("row_0", "row_1", "col_0", "col_1")
ROW_COL = AXES
ROW = AXES[:2]
COL = AXES[2:]
NY, NK, NZ, NX = 4, 2, 8, 4
NR = NY * NK
BLK = 128
OWN = 512
LOC = 1024
NEV = 64
RHS = 32
LANES = 128
PART = 2048
CHUNKS = 4
WIDTH = PART // CHUNKS
ROWS = WIDTH // LANES
F32 = jnp.float32
BF16 = jnp.bfloat16
NT = (((1,), (1,)), ((), ()))


def away(d, n):
    return min(d, n - d)


FAR_YKX = sorted(
    ((dy, dk, dx) for dy in range(NY) for dk in range(NK) for dx in range(NX) if (dy, dk, dx) != (0, 0, 0)),
    key=lambda d: -away(d[0], NY) - away(d[2], NX))
FAR_ZX = sorted(
    ((dz, dx) for dz in range(NZ) for dx in range(NX) if (dz, dx) != (0, 0)), key=lambda d: -away(d[0], NZ) - away(d[1], NX))
FAR_YK = sorted(((dy, dk) for dy in range(NY) for dk in range(NK) if (dy, dk) != (0, 0)), key=lambda d: -away(d[0], NY))
FAR_Z = sorted(range(1, NZ), key=lambda d: -away(d, NZ))
FAR_X = sorted(range(1, NX), key=lambda d: -away(d, NX))


def dot(a, b):
    return jnp.dot(a, b, preferred_element_type=F32)


def dot_nt(a, b):
    return lax.dot_general(a, b, NT, preferred_element_type=F32)


def halves(x):
    high = x.astype(BF16)
    return high, (x - high.astype(F32)).astype(BF16)


def kernel(
    ib, resid_hbm, slots_hbm, basis_hbm, linv_hbm, cinv_hbm, out,
    resid, slots, basis, linv, cinv, chigh, clow, bstack, hout, hin, psend, precv, table, pick1, pick2,
    gsend, grecv, xsend, xrecv, zsend, zrecv, table2, osend, orecv, rsend, rrecv,
    load_sem, send_sem, recv_sem, xsem,
):
    y, k, z, x = (lax.axis_index(a) for a in AXES)
    r = y * NK + k
    c = z * NX + x
    ys = [lax.rem(y + d, NY) for d in range(NY)]
    ks = [lax.rem(k + d, NK) for d in range(NK)]
    zs = [lax.rem(z + d, NZ) for d in range(NZ)]
    xs = [lax.rem(x + d, NX) for d in range(NX)]

    def at_rx(r2, x2):
        return (lax.div(r2, NK), lax.rem(r2, NK), z, x2)

    def at_zx(z2, x2):
        return (y, k, z2, x2)

    def send(stage, src, dst, where, sem=None):
        pltpu.make_async_remote_copy(
            src_ref=src, dst_ref=dst, send_sem=send_sem.at[stage], recv_sem=recv_sem.at[stage] if sem is None else sem,
            device_id=where, device_id_type=MESH,
        ).start()

    def landed(ref, sem):
        pltpu.make_async_copy(ref, ref, sem).wait()

    loads = [
        pltpu.make_async_copy(resid_hbm, resid, load_sem.at[0]),
        pltpu.make_async_copy(basis_hbm, basis, load_sem.at[1]),
        pltpu.make_async_copy(slots_hbm, slots, load_sem.at[2]),
        pltpu.make_async_copy(linv_hbm, linv, load_sem.at[3]),
        pltpu.make_async_copy(cinv_hbm, cinv, load_sem.at[4]),
    ]
    loads[0].start()
    barrier = pltpu.get_barrier_semaphore()
    for dz, dx in FAR_ZX:
        if dz > 0:
            pl.semaphore_signal(barrier, inc=1, device_id=at_zx(zs[dz], xs[dx]), device_id_type=MESH)
    for dy, dk, dx in FAR_YKX:
        pl.semaphore_signal(barrier, inc=1, device_id=(ys[dy], ks[dk], z, xs[dx]), device_id_type=MESH)
    for load in loads[1:]:
        load.start()

    loads[0].wait()
    blocks = [resid[:, b * BLK:(b + 1) * BLK] for b in range(OWN // BLK)]
    for d in range(4):
        which = ib[0, d]
        block = blocks[0]
        for b in range(1, OWN // BLK):
            block = jnp.where(which == b, blocks[b], block)
        hout[d] = block

    loads[1].wait()
    bhigh, blow = halves(basis[...])
    for half in range(2):
        bstack[2 * half * NEV:(2 * half + 1) * NEV] = bhigh
        bstack[(2 * half + 1) * NEV:(2 * half + 2) * NEV] = blow

    pl.semaphore_wait(barrier, NR * NX - 1 + (NZ - 1) * NX)

    r_up, r_down = lax.rem(r + 1, NR), lax.rem(r + NR - 1, NR)
    c_up, c_down = lax.rem(c + 1, NZ * NX), lax.rem(c + NZ * NX - 1, NZ * NX)
    sides = (
        at_rx(r_up, x), at_rx(r_down, x),
        at_zx(lax.div(c_up, NX), lax.rem(c_up, NX)), at_zx(lax.div(c_down, NX), lax.rem(c_down, NX)),
    )
    inside = (r > 0, r < NR - 1, c > 0, c < NZ * NX - 1)
    inside_back = (r < NR - 1, r > 0, c < NZ * NX - 1, c > 0)
    for d in range(4):
        send(0, hout.at[d], hin.at[d], sides[d])

    own = dot_nt(resid[...], bstack[:2 * NEV, :OWN])
    sub = lax.broadcasted_iota(jnp.int32, (LANES, LANES), 0)
    loads[2].wait()
    my_slots = slots[pl.ds(r * 16, 16), :]
    want_row, want_lane = lax.shift_right_logical(my_slots, 7), my_slots & (LANES - 1)

    landed(hin, recv_sem.at[0])
    halo = jnp.concatenate([jnp.where(inside[d], hin[d], jnp.zeros_like(hin[d])) for d in range(4)], axis=1)

    split2 = own + dot_nt(halo, bstack[:2 * NEV, OWN:])
    psend[...] = (split2 + pltpu.roll(split2, NEV, 1)).reshape(RHS, 1, LANES)
    me = r * NX + x
    precv[pl.ds(me, 1)] = psend[pl.ds(me, 1)]
    group = [((ys[dy], ks[dk], z, xs[dx]), (ys[dy] * NK + ks[dk]) * NX + xs[dx], xs[dx]) for dy, dk, dx in FAR_YKX]
    for where, index, _ in group:
        send(1, psend.at[index], precv.at[me], where)

    sub16 = lax.broadcasted_iota(jnp.int32, (16, LANES), 0)
    lane16 = lax.broadcasted_iota(jnp.int32, (16, LANES), 1).astype(F32)

    def invert(g, total):
        rows = slots[pl.ds(g * 8, 8), :]
        low = rows & (LANES - 1)
        high = lax.shift_right_logical(rows, 7) - z * 16
        picks, values = [], []
        for u in range(8):
            entry = g * 8 + u
            row = lax.rem(lax.div(entry, 2), NZ) * 16 + lax.div(entry, 16) * 2 + (u & 1)
            picks.append((low[u:u + 1] == sub).astype(F32).astype(BF16))
            here = high[u:u + 1] == sub16
            values.append(jnp.concatenate(
                [jnp.where(here, row.astype(F32), 0.0), jnp.where(here, lane16, 0.0)], axis=0).astype(BF16))
        return total + dot_nt(jnp.concatenate(picks, axis=1), jnp.concatenate(values, axis=1))

    def one_hot(pick, row):
        for a in range(16):
            hot = (row[a:a + 1] == sub).astype(F32).astype(BF16)
            pick[:LANES, a * LANES:(a + 1) * LANES] = hot
            pick[LANES:, a * LANES:(a + 1) * LANES] = hot

    inverse = lax.fori_loop(0, 16, invert, jnp.zeros((LANES, 32), F32)).T.astype(jnp.int32)
    from_row, from_lane = inverse[:16], inverse[16:]
    one_hot(pick1, from_row)

    def gather(source, pick, lane):
        high, low = halves(source.T)
        stacked = jnp.concatenate([high, low], axis=1)
        rows = []
        for a in range(0, 16, 2):
            picked = dot(stacked, pick[:, a * LANES:(a + 2) * LANES])
            for h in range(2):
                mine = lane[a + h:a + h + 1] == sub
                rows.append(jnp.sum(jnp.where(mine, picked[:, h * LANES:(h + 1) * LANES], 0.0), axis=0, keepdims=True))
        return jnp.concatenate(rows, axis=0)

    landed(precv.at[pl.ds(0, NR * NX - 1)], recv_sem.at[1])

    got = precv[...].reshape(16, 2, LANES)
    first = lax.broadcasted_iota(jnp.int32, (16, LANES), 1) < NEV
    mine = pl.ds(pl.multiple_of(z * 16, 16), 16)
    table[mine, :] = jnp.where(first, got[:, 0], got[:, 1])
    for dz in FAR_Z:
        send(2, table.at[mine], table.at[mine], at_zx(zs[dz], x))

    loads[3].wait()
    schwarz = dot_nt(resid[...], linv[:, :OWN]) + dot_nt(halo, linv[:, OWN:])
    loads[4].wait()

    def split(i, _):
        rows = pl.ds(i * 64, 64)
        high, low = halves(cinv[rows, :])
        chigh[rows, :] = high
        clow[rows, :] = low
        return 0

    lax.fori_loop(0, PART // 128, split, 0)

    landed(table.at[pl.ds(0, (NZ - 1) * 16)], recv_sem.at[2])

    gsend[...] = gather(table[...], pick1, from_lane).reshape(NX, 4, LANES)
    grecv[pl.ds(me, 1)] = gsend[pl.ds(x, 1)]
    for where, _, x2 in group:
        send(3, gsend.at[x2], grecv.at[me], where)

    lax.fori_loop(PART // 128, PART // 64, split, 0)

    landed(grecv.at[pl.ds(0, NR * NX - 1)], recv_sem.at[3])

    rhigh, rlow = halves(jnp.concatenate([grecv[:, a, :] for a in range(4)], axis=1))
    both = jnp.concatenate([rhigh, rlow], axis=0)
    for n in range(CHUNKS):
        for i in range(WIDTH // 256):
            rows = pl.ds(n * WIDTH + i * 256, 256)
            top = dot_nt(both, chigh[rows, :])
            part = top[:RHS] + top[RHS:] + dot_nt(rhigh, clow[rows, :])
            xsend[n, :, :, i * 256:(i + 1) * 256] = part.reshape(NX, NZ, 256)
        for dx in FAR_X:
            send(4, xsend.at[n, xs[dx]], xrecv.at[n, dx - 1], at_zx(z, xs[dx]), xsem.at[n])

    one_hot(pick2, want_row)

    for n in range(CHUNKS):
        landed(xrecv.at[n], xsem.at[n])
        total = xsend[n, pl.ds(x, 1)][0]
        for p in range(NX - 1):
            total = total + xrecv[n, p]
        for j in range(ROWS):
            zsend[n, :, j, :] = total[:, j * LANES:(j + 1) * LANES]
        for dz in FAR_Z:
            send(5, zsend.at[n, zs[dz]], zrecv.at[dz - 1, n], at_zx(zs[dz], x))

    landed(zrecv, recv_sem.at[5])
    mine2 = pl.ds(pl.multiple_of(r * 16, 16), 16)
    total = zsend[:, pl.ds(z, 1)].reshape(16, LANES)
    for p in range(NZ - 1):
        total = total + zrecv[p].reshape(16, LANES)
    table2[mine2, :] = total

    for dy, dk in FAR_YK:
        send(6, table2.at[mine2], table2.at[mine2], (ys[dy], ks[dk], z, x))

    landed(table2.at[pl.ds(0, (NR - 1) * 16)], recv_sem.at[6])

    osend[...] = gather(table2[...], pick2, want_lane).reshape(16, 1, LANES)
    q = x * NZ + z
    orecv[pl.ds(q, 1)] = osend[pl.ds(lax.div(c, 2), 1)]
    for dz, dx in FAR_ZX:
        send(7, osend.at[zs[dz] * 2 + lax.div(xs[dx], 2)], orecv.at[q], at_zx(zs[dz], xs[dx]))

    landed(orecv.at[pl.ds(0, NZ * NX - 1)], recv_sem.at[7])
    entries = orecv[...].reshape(RHS, LANES)
    high, low = halves(jnp.where(lax.rem(x, 2) == 1, entries[:, NEV:], entries[:, :NEV]))
    coarse = jnp.concatenate([high, high, low, low], axis=1)

    back = dot(coarse, bstack[:, OWN:])
    for d in range(4):
        rsend[d] = back[:, d * BLK:(d + 1) * BLK]
    opposite = (1, 0, 3, 2)
    for d in range(4):
        send(8, rsend.at[d], rrecv.at[d], sides[opposite[d]])
    result = schwarz + dot(coarse, bstack[:, :OWN])
    landed(rrecv, recv_sem.at[8])
    parts = [result[:, b * BLK:(b + 1) * BLK] for b in range(OWN // BLK)]
    for d in range(4):
        returned = jnp.where(inside_back[d], rrecv[d], jnp.zeros_like(rrecv[d]))
        which = ib[0, d]
        for b in range(OWN // BLK):
            parts[b] = parts[b] + jnp.where(which == b, returned, jnp.zeros_like(returned))
    for b in range(OWN // BLK):
        out[:, b * BLK:(b + 1) * BLK] = parts[b]

    for stage, ref in (
        (0, hout), (1, psend.at[pl.ds(0, NR * NX - 1)]), (2, table.at[pl.ds(0, (NZ - 1) * 16)]),
        (3, grecv.at[pl.ds(0, NR * NX - 1)]), (4, xrecv), (5, zrecv), (6, table2.at[pl.ds(0, (NR - 1) * 16)]),
        (7, orecv.at[pl.ds(0, NZ * NX - 1)]), (8, rsend),
    ):
        landed(ref, send_sem.at[stage])


def local(residuals, intersect_blocks, local_inverse, coarse_basis, coarse_slots, coarse_inverse):
    vmem = pl.BlockSpec(memory_space=pltpu.VMEM)
    hbm = pl.BlockSpec(memory_space=pl.ANY)
    arrays = (
        intersect_blocks, residuals.T, coarse_slots.reshape(LANES, LANES), coarse_basis.T, local_inverse, coarse_inverse
    )
    result = pl.pallas_call(
        kernel,
        out_shape=jax.ShapeDtypeStruct((RHS, OWN), F32),
        in_specs=[pl.BlockSpec(memory_space=pltpu.SMEM)] + [hbm] * 5,
        out_specs=vmem,
        scratch_shapes=[
            pltpu.VMEM((RHS, OWN), BF16),
            pltpu.VMEM((LANES, LANES), jnp.int32),
            pltpu.VMEM((NEV, LOC), F32),
            pltpu.VMEM((OWN, LOC), BF16),
            pltpu.VMEM((PART, OWN), F32),
            pltpu.VMEM((PART, OWN), BF16),
            pltpu.VMEM((PART, OWN), BF16),
            pltpu.VMEM((4 * NEV, LOC), BF16),
            pltpu.VMEM((4, RHS, BLK), BF16),
            pltpu.VMEM((4, RHS, BLK), BF16),
            pltpu.VMEM((RHS, 1, LANES), F32),
            pltpu.VMEM((RHS, 1, LANES), F32),
            pltpu.VMEM((LANES, LANES), F32),
            pltpu.VMEM((2 * LANES, PART), BF16),
            pltpu.VMEM((2 * LANES, PART), BF16),
            pltpu.VMEM((NX, 4, LANES), F32),
            pltpu.VMEM((RHS, 4, LANES), F32),
            pltpu.VMEM((CHUNKS, NX, NZ, WIDTH), F32),
            pltpu.VMEM((CHUNKS, NX - 1, NZ, WIDTH), F32),
            pltpu.VMEM((CHUNKS, NZ, ROWS, LANES), F32),
            pltpu.VMEM((NZ - 1, CHUNKS, ROWS, LANES), F32),
            pltpu.VMEM((LANES, LANES), F32),
            pltpu.VMEM((16, 1, LANES), F32),
            pltpu.VMEM((RHS, 1, LANES), F32),
            pltpu.VMEM((4, RHS, BLK), F32),
            pltpu.VMEM((4, RHS, BLK), F32),
            pltpu.SemaphoreType.DMA((5,)),
            pltpu.SemaphoreType.DMA((9,)),
            pltpu.SemaphoreType.DMA((9,)),
            pltpu.SemaphoreType.DMA((CHUNKS,)),
        ],
        compiler_params=pltpu.CompilerParams(collective_id=0, has_side_effects=True, vmem_limit_bytes=32 * 2**20),
        name="schwarz",
    )(*(pltpu.with_memory_space_constraint(array, pltpu.HBM) for array in arrays))
    return result.T


def solution(mesh):
    torus = Mesh(mesh.devices.reshape(NY, NK, NZ, NX), AXES)
    in_specs = (
        P(ROW_COL, None),
        P(ROW_COL, None),
        P(ROW_COL, None),
        P(ROW_COL, None),
        P(),
        P(ROW, COL),
    )
    return jax.shard_map(local, mesh=torus, in_specs=in_specs, out_specs=P(ROW_COL, None), check_vma=False)
```

time: 60.3 us -> 54.8 us (0.909)
  Pallas kernels: 58.7 us -> 54 us
  local copies, waits for them, and re-layouts: 1.47 us -> 0.63 us
    pallas_call x1, Pallas kernels: 58.7 us -> 54 us  [local(): pl.pallas_call(kernel, out_shape=jax.ShapeDtypeStruct((RHS, OWN), F32), i...]
    unnamed x1, local copies, waits for them, and re-layouts: 1.47 us -> 0.63 us
where the time goes in v2:
time: 54.8 us; the launch traced here: 54.6 us
  Pallas kernels  54 us (99%)
  local copies, waits for them, and re-layouts  0.63 us (1%)
    pallas_call x1, Pallas kernels, local(): pl.pallas_call(kernel, out_shape=jax.ShapeDtypeStruct((RHS, OWN), F32), i...  54 us

profile of v2, /device:TPU:1, one launch (start us, length us, event | category | flops | bytes accessed | tf_op | source)
XLA Modules:
  0.0 54.6 jit_solution(15862408420669570319)
XLA Ops:
  0.0 54.0 %schwarz.1 = f32[32,512]{1,0:T(8,128)S(1)} custom-call(s32[1,4]{1,0:T(1,128)} %ib.1, bf16[32,512]{1,0:T(8,128)(2,1)} %bitcast.7, s32[128,128]{1,0:T(8,128)} %bitcast.6, f32[64,1024]{1,0:T(8,128)} %bitcast.5, bf16[512,1024]{1,0:T(8,128)(2,1)} %linv_hbm.1, f32[2048,512]{1,0:T(8,128)} %cinv_hbm.1), custom_call_target="tpu_custom_call" | custom-call | tf_op jit(solution)/shard_map/schwarz/pallas_call | solution.py:299
  54.0 0.6 %copy.8 = f32[512,32]{0,1:T(8,128)} copy(f32[512,32]{0,1:T(8,128)S(1)} %bitcast.4) | data formatting | bytes 131072

commit v3 on v2

--- a/solution.py
+++ b/solution.py
@@ -58,9 +58,9 @@
 
 
 def kernel(
-    ib, resid_hbm, slots_hbm, basis_hbm, linv_hbm, cinv_hbm, out,
-    resid, slots, basis, linv, cinv, chigh, clow, bstack, hout, hin, psend, precv, table, pick1, pick2,
-    gsend, grecv, xsend, xrecv, zsend, zrecv, table2, osend, orecv, rsend, rrecv,
+    ib_hbm, resid_hbm, slots_hbm, basis_hbm, linv_hbm, cinv_hbm, out,
+    ib, resid, slots, basis, linv, cinv, chigh, clow, bstack, hout, hin, psend, precv, table, pick1, pick2,
+    gsend, grecv, xsend, xrecv, zsend, zrecv, table2, osend, orecv, nrecv, nbasis,
     load_sem, send_sem, recv_sem, xsem,
 ):
     y, k, z, x = (lax.axis_index(a) for a in AXES)
@@ -92,18 +92,29 @@
         pltpu.make_async_copy(slots_hbm, slots, load_sem.at[2]),
         pltpu.make_async_copy(linv_hbm, linv, load_sem.at[3]),
         pltpu.make_async_copy(cinv_hbm, cinv, load_sem.at[4]),
+        pltpu.make_async_copy(ib_hbm, ib, load_sem.at[5]),
     ]
     loads[0].start()
+    loads[5].start()
     barrier = pltpu.get_barrier_semaphore()
-    for dz, dx in FAR_ZX:
-        if dz > 0:
-            pl.semaphore_signal(barrier, inc=1, device_id=at_zx(zs[dz], xs[dx]), device_id_type=MESH)
+    for dz in FAR_Z:
+        pl.semaphore_signal(barrier, inc=1, device_id=at_zx(zs[dz], x), device_id_type=MESH)
     for dy, dk, dx in FAR_YKX:
         pl.semaphore_signal(barrier, inc=1, device_id=(ys[dy], ks[dk], z, xs[dx]), device_id_type=MESH)
-    for load in loads[1:]:
+
+    @pl.when(x == NX - 1)
+    def _():
+        pl.semaphore_signal(barrier, inc=1, device_id=at_zx(zs[1], 0), device_id_type=MESH)
+
+    @pl.when(x == 0)
+    def _():
+        pl.semaphore_signal(barrier, inc=1, device_id=at_zx(zs[NZ - 1], NX - 1), device_id_type=MESH)
+
+    for load in loads[1:5]:
         load.start()
 
     loads[0].wait()
+    loads[5].wait()
     blocks = [resid[:, b * BLK:(b + 1) * BLK] for b in range(OWN // BLK)]
     for d in range(4):
         which = ib[0, d]
@@ -114,11 +125,12 @@
 
     loads[1].wait()
     bhigh, blow = halves(basis[...])
-    for half in range(2):
-        bstack[2 * half * NEV:(2 * half + 1) * NEV] = bhigh
-        bstack[(2 * half + 1) * NEV:(2 * half + 2) * NEV] = blow
-
-    pl.semaphore_wait(barrier, NR * NX - 1 + (NZ - 1) * NX)
+    bstack[:NEV] = bhigh
+    bstack[NEV:] = blow
+    osend[0] = jnp.zeros((1, LANES), F32)
+    osend[17] = jnp.zeros((1, LANES), F32)
+
+    pl.semaphore_wait(barrier, NR * NX - 1 + NZ - 1 + jnp.where(x == NX - 1, 1, 0) + jnp.where(x == 0, 1, 0))
 
     r_up, r_down = lax.rem(r + 1, NR), lax.rem(r + NR - 1, NR)
     c_up, c_down = lax.rem(c + 1, NZ * NX), lax.rem(c + NZ * NX - 1, NZ * NX)
@@ -131,7 +143,7 @@
     for d in range(4):
         send(0, hout.at[d], hin.at[d], sides[d])
 
-    own = dot_nt(resid[...], bstack[:2 * NEV, :OWN])
+    own = dot_nt(resid[...], bstack[:, :OWN])
     sub = lax.broadcasted_iota(jnp.int32, (LANES, LANES), 0)
     loads[2].wait()
     my_slots = slots[pl.ds(r * 16, 16), :]
@@ -140,13 +152,16 @@
     landed(hin, recv_sem.at[0])
     halo = jnp.concatenate([jnp.where(inside[d], hin[d], jnp.zeros_like(hin[d])) for d in range(4)], axis=1)
 
-    split2 = own + dot_nt(halo, bstack[:2 * NEV, OWN:])
+    split2 = own + dot_nt(halo, bstack[:, OWN:])
     psend[...] = (split2 + pltpu.roll(split2, NEV, 1)).reshape(RHS, 1, LANES)
     me = r * NX + x
     precv[pl.ds(me, 1)] = psend[pl.ds(me, 1)]
     group = [((ys[dy], ks[dk], z, xs[dx]), (ys[dy] * NK + ks[dk]) * NX + xs[dx], xs[dx]) for dy, dk, dx in FAR_YKX]
     for where, index, _ in group:
         send(1, psend.at[index], precv.at[me], where)
+
+    for d in range(4):
+        send(8, bstack.at[:, pl.ds(OWN + d * BLK, BLK)], nbasis.at[d], sides[(1, 0, 3, 2)[d]])
 
     sub16 = lax.broadcasted_iota(jnp.int32, (16, LANES), 0)
     lane16 = lax.broadcasted_iota(jnp.int32, (16, LANES), 1).astype(F32)
@@ -254,28 +269,38 @@
 
     landed(table2.at[pl.ds(0, (NR - 1) * 16)], recv_sem.at[6])
 
-    osend[...] = gather(table2[...], pick2, want_lane).reshape(16, 1, LANES)
+    osend[1:17] = gather(table2[...], pick2, want_lane).reshape(16, 1, LANES)
     q = x * NZ + z
-    orecv[pl.ds(q, 1)] = osend[pl.ds(lax.div(c, 2), 1)]
-    for dz, dx in FAR_ZX:
-        send(7, osend.at[zs[dz] * 2 + lax.div(xs[dx], 2)], orecv.at[q], at_zx(zs[dz], xs[dx]))
-
+    orecv[pl.ds(q, 1)] = osend[pl.ds(z * 2 + lax.div(x + 1, 2), 2)].reshape(1, 2, 1, LANES)
+    y_up, k_up = lax.div(r_up, NK), lax.rem(r_up, NK)
+    y_down, k_down = lax.div(r_down, NK), lax.rem(r_down, NK)
+    for dz, dx in FAR_ZX + [(0, 0)]:
+        pair = osend.at[zs[dz] * 2 + lax.div(xs[dx], 2) + 1]
+        send(9, pair, nrecv.at[0, q], (y_down, k_down, zs[dz], xs[dx]))
+        send(9, pair, nrecv.at[1, q], (y_up, k_up, zs[dz], xs[dx]))
+        if (dz, dx) != (0, 0):
+            send(7, osend.at[pl.ds(zs[dz] * 2 + lax.div(xs[dx] + 1, 2), 2)], orecv.at[q], at_zx(zs[dz], xs[dx]))
+
+    landed(nbasis, recv_sem.at[8])
     landed(orecv.at[pl.ds(0, NZ * NX - 1)], recv_sem.at[7])
-    entries = orecv[...].reshape(RHS, LANES)
-    high, low = halves(jnp.where(lax.rem(x, 2) == 1, entries[:, NEV:], entries[:, :NEV]))
-    coarse = jnp.concatenate([high, high, low, low], axis=1)
-
-    back = dot(coarse, bstack[:, OWN:])
-    for d in range(4):
-        rsend[d] = back[:, d * BLK:(d + 1) * BLK]
-    opposite = (1, 0, 3, 2)
-    for d in range(4):
-        send(8, rsend.at[d], rrecv.at[d], sides[opposite[d]])
-    result = schwarz + dot(coarse, bstack[:, :OWN])
-    landed(rrecv, recv_sem.at[8])
+    landed(nrecv, recv_sem.at[9])
+
+    def prolonged(entries, vectors):
+        high, low = halves(entries)
+        stacked = jnp.concatenate([jnp.concatenate([part, part], axis=1) for part in (high, low)], axis=0)
+        both = dot(stacked, vectors)
+        return both[:RHS] + both[RHS:]
+
+    odd = lax.rem(x, 2) == 1
+    pairs = jnp.concatenate([orecv[:, h].reshape(RHS, LANES) for h in range(2)], axis=1)
+    line = jnp.where(odd, pairs[:, :3 * NEV], pairs[:, NEV:])
+    beside = [nrecv[h].reshape(RHS, LANES) for h in range(2)]
+    sources = [jnp.where(odd, pair[:, NEV:], pair[:, :NEV]) for pair in beside] + [line[:, 2 * NEV:], line[:, :NEV]]
+    result = schwarz + prolonged(line[:, NEV:2 * NEV], bstack[:, :OWN])
     parts = [result[:, b * BLK:(b + 1) * BLK] for b in range(OWN // BLK)]
     for d in range(4):
-        returned = jnp.where(inside_back[d], rrecv[d], jnp.zeros_like(rrecv[d]))
+        returned = prolonged(sources[d], nbasis[d])
+        returned = jnp.where(inside_back[d], returned, jnp.zeros_like(returned))
         which = ib[0, d]
         for b in range(OWN // BLK):
             parts[b] = parts[b] + jnp.where(which == b, returned, jnp.zeros_like(returned))
@@ -285,7 +310,7 @@
     for stage, ref in (
         (0, hout), (1, psend.at[pl.ds(0, NR * NX - 1)]), (2, table.at[pl.ds(0, (NZ - 1) * 16)]),
         (3, grecv.at[pl.ds(0, NR * NX - 1)]), (4, xrecv), (5, zrecv), (6, table2.at[pl.ds(0, (NR - 1) * 16)]),
-        (7, orecv.at[pl.ds(0, NZ * NX - 1)]), (8, rsend),
+        (7, orecv.at[pl.ds(0, NZ * NX - 1)]), (8, nbasis), (9, nrecv),
     ):
         landed(ref, send_sem.at[stage])
 
@@ -299,9 +324,10 @@
     result = pl.pallas_call(
         kernel,
         out_shape=jax.ShapeDtypeStruct((RHS, OWN), F32),
-        in_specs=[pl.BlockSpec(memory_space=pltpu.SMEM)] + [hbm] * 5,
+        in_specs=[hbm] * 6,
         out_specs=vmem,
         scratch_shapes=[
+            pltpu.SMEM((1, 4), jnp.int32),
             pltpu.VMEM((RHS, OWN), BF16),
             pltpu.VMEM((LANES, LANES), jnp.int32),
             pltpu.VMEM((NEV, LOC), F32),
@@ -309,7 +335,7 @@
             pltpu.VMEM((PART, OWN), F32),
             pltpu.VMEM((PART, OWN), BF16),
             pltpu.VMEM((PART, OWN), BF16),
-            pltpu.VMEM((4 * NEV, LOC), BF16),
+            pltpu.VMEM((2 * NEV, LOC), BF16),
             pltpu.VMEM((4, RHS, BLK), BF16),
             pltpu.VMEM((4, RHS, BLK), BF16),
             pltpu.VMEM((RHS, 1, LANES), F32),
@@ -324,13 +350,13 @@
             pltpu.VMEM((CHUNKS, NZ, ROWS, LANES), F32),
             pltpu.VMEM((NZ - 1, CHUNKS, ROWS, LANES), F32),
             pltpu.VMEM((LANES, LANES), F32),
-            pltpu.VMEM((16, 1, LANES), F32),
-            pltpu.VMEM((RHS, 1, LANES), F32),
-            pltpu.VMEM((4, RHS, BLK), F32),
-            pltpu.VMEM((4, RHS, BLK), F32),
-            pltpu.SemaphoreType.DMA((5,)),
-            pltpu.SemaphoreType.DMA((9,)),
-            pltpu.SemaphoreType.DMA((9,)),
+            pltpu.VMEM((18, 1, LANES), F32),
+            pltpu.VMEM((RHS, 2, 1, LANES), F32),
+            pltpu.VMEM((2, RHS, 1, LANES), F32),
+            pltpu.VMEM((4, 2 * NEV, BLK), BF16),
+            pltpu.SemaphoreType.DMA((6,)),
+            pltpu.SemaphoreType.DMA((10,)),
+            pltpu.SemaphoreType.DMA((10,)),
             pltpu.SemaphoreType.DMA((CHUNKS,)),
         ],
         compiler_params=pltpu.CompilerParams(collective_id=0, has_side_effects=True, vmem_limit_bytes=32 * 2**20),

time: 54.8 us -> 50.9 us (0.929)
  Pallas kernels: 54 us -> 50.2 us
    pallas_call x1, Pallas kernels: 54 us -> 50.2 us  [local(): pl.pallas_call(kernel, out_shape=jax.ShapeDtypeStruct((RHS, OWN), F32), i...]
where the time goes in v3:
time: 50.9 us; the launch traced here: 50.8 us
  Pallas kernels  50.2 us (99%)
  local copies, waits for them, and re-layouts  0.63 us (1%)
    pallas_call x1, Pallas kernels, local(): pl.pallas_call(kernel, out_shape=jax.ShapeDtypeStruct((RHS, OWN), F32), i...  50.2 us

profile of v3, /device:TPU:1, one launch (start us, length us, event | category | flops | bytes accessed | tf_op | source)
XLA Modules:
  0.0 50.8 jit_solution(2926890484751554688)
XLA Ops:
  0.0 50.2 %schwarz.1 = f32[32,512]{1,0:T(8,128)S(1)} custom-call(s32[1,4]{1,0:T(1,128)} %ib_hbm.1, bf16[32,512]{1,0:T(8,128)(2,1)} %bitcast.7, s32[128,128]{1,0:T(8,128)} %bitcast.6, f32[64,1024]{1,0:T(8,128)} %bitcast.5, bf16[512,1024]{1,0:T(8,128)(2,1)} %linv_hbm.1, f32[2048,512]{1,0:T(8,128)} %cinv_hbm.1), custom_call_target="tpu_custom_call" | custom-call | tf_op jit(solution)/shard_map/schwarz/pallas_call | solution.py:324
  50.2 0.6 %copy.8 = f32[512,32]{0,1:T(8,128)} copy(f32[512,32]{0,1:T(8,128)S(1)} %bitcast.4) | data formatting | bytes 131072
